TPU v7x, 1024 devices: a whole 8x8x8 slice. The times are simulated.
1024 devices in a mesh: mem: 16 (over x_hi, y), band: 64 (over x_lo, z, core).
Axes of the slice: x: 8 (x_hi: 2, x_lo: 4; x = x_hi * 4 + x_lo), y: 8, z: 8, core: 2. Of those that a mesh axis runs over, the one named last changes fastest.
Arguments:
- prior_collection: float32 [512, 3, 512, 256], P('mem', None, 'band'), may hold values from -3 to 3
- obs_index: int32 [64, 16, 256], P('band'), may hold values from 0 to 1151
- obs_values: float32 [64, 16, 256], P('band', 'mem'), may hold values from -6 to 6
- obs_var: float32 [64, 16, 256], P('band', 'mem'), may hold values from 0.1 to 1
Outputs:
- analysis: float32 [512, 3, 512, 256], P('mem', None, 'band')
Inputs may be any that keep to these rules, and one draw needn't show every extreme that they name: obs_index[b, p, i] is field * 3 * 8 * 16 + row * 3 * 16 + c, a position in the window of patch p of band b.
All inputs are finite; a program needn't handle non-finite values. Where the computation divides by a largest or mean magnitude, that divisor is 1e-20 or more.
Results may differ from a plain program's by a relative error of at most 0.0022.
Values may be sent and summed in bfloat16 or wider, within the bound.
No kernel may reach another device: no remote copies, remote signals or barrier semaphores. Data moves between devices by JAX's collectives and lax.ppermute only.
A program may use at most 64 MiB of HBM per device.

v0:
```python
import math

import jax
import jax.numpy as jnp
from jax import lax
from jax.experimental import pallas as pl
from jax.experimental.pallas import tpu as pltpu
from jax.sharding import PartitionSpec as P

STEPS = 3
NEWTON = 3
HALO = 2 * STEPS

time_step = 0.1
gravity = 1.0
coriolis = 0.05
mean_depth = 1.0

GROUP = 8
LANES = 128
BLOCK = 16


def tiled_view(x):
    m, f, r, c = x.shape
    halves = c // LANES
    return x.reshape(m, f, r, halves, LANES).transpose(0, 1, 3, 2, 4).reshape(-1, LANES)


def untiled_view(x, shape):
    m, f, r, c = shape
    halves = c // LANES
    return x.reshape(m, f, halves, r, LANES).transpose(0, 1, 3, 2, 4).reshape(shape)


def block_transpose(tiles):
    tiles = list(tiles)
    block = lax.broadcasted_iota(jnp.int32, tiles[0].shape, 1) // BLOCK
    for s in (4, 2, 1):
        high = (block & s) != 0
        for i in range(8):
            if i & s:
                continue
            a, b = tiles[i], tiles[i + s]
            tiles[i] = jnp.where(high, pltpu.roll(b, BLOCK * s, 1), a)
            tiles[i + s] = jnp.where(high, b, pltpu.roll(a, LANES - BLOCK * s, 1))
    return tiles


def edges_kernel(prior_ref, first_ref, last_ref):
    fields, rows = 3, 8
    stride = fields * rows * 2
    for member in range(0, first_ref.shape[1], 2 * GROUP):
        for f in range(fields):
            for half in range(2):
                lanes = slice(half * LANES, (half + 1) * LANES)
                for row in range(rows):
                    parts = [
                        prior_ref[pl.ds((m * fields + f) * 2 * rows + half * rows + row, GROUP, stride=stride), :]
                        for m in (member, member + GROUP)
                    ]
                    both = jnp.concatenate(parts, axis=0).astype(jnp.bfloat16)
                    if row < HALO:
                        first_ref[f * HALO + row, member : member + 2 * GROUP, lanes] = both
                    if row >= rows - HALO:
                        last_ref[f * HALO + row - (rows - HALO), member : member + 2 * GROUP, lanes] = both


def east_west(x):
    cols = x.shape[-1]
    return (pltpu.roll(x, cols - 1, 1) - pltpu.roll(x, 1, 1)) * 0.5


def forecast_kernel(inside_ref, prior_ref, above_ref, below_ref, index_ref, state_ref, observed_ref, ping, pong, window):
    fields, rows = 3, 8
    deep = rows + 2 * HALO
    stride = fields * rows * 2
    members = state_ref.shape[1]
    patches = state_ref.shape[0]
    above_in = inside_ref[0]
    below_in = inside_ref[1]

    for f in range(fields):
        for row in range(HALO):
            ping[f * deep + row] = above_ref[f * HALO + row].astype(jnp.float32)
            ping[f * deep + HALO + rows + row] = below_ref[f * HALO + row].astype(jnp.float32)

    for member in range(0, members, GROUP):
        here = slice(member, member + GROUP)
        for f in range(fields):
            for half in range(2):
                for row in range(rows):
                    start = (member * fields + f) * 2 * rows + half * rows + row
                    ping[f * deep + HALO + row, here, half * LANES : (half + 1) * LANES] = prior_ref[
                        pl.ds(start, GROUP, stride=stride), :
                    ]

    def one_group(g, carry):
        here = pl.ds(pl.multiple_of(g * GROUP, GROUP), GROUP)

        def masked(x, row):
            if row < HALO:
                return x * above_in
            if row >= HALO + rows:
                return x * below_in
            return x

        src, dst = ping, pong
        for turn in range(STEPS):
            low = 2 * (turn + 1)
            high = deep - 2 * (turn + 1)

            def get(f, row, src=src):
                return src[f * deep + row, here, :]

            north_flux = {}

            def flux(row, get=get, north_flux=north_flux):
                if row not in north_flux:
                    north_flux[row] = (mean_depth + get(0, row)) * get(2, row)
                return north_flux[row]

            def new_height(row, get=get, flux=flux):
                height = get(0, row)
                flux_east = (mean_depth + height) * get(1, row)
                value = height - time_step * (
                    east_west(flux_east) + (flux(row + 1) - flux(row - 1)) * 0.5
                )
                return masked(value, row)

            heights = {row: new_height(row) for row in (low - 1, low)}
            for row in range(low, high):
                heights[row + 1] = new_height(row + 1)
                east = get(1, row)
                north = get(2, row)
                east_slope = (get(1, row + 1) - get(1, row - 1)) * 0.5
                north_slope = (get(2, row + 1) - get(2, row - 1)) * 0.5
                height_slope = (heights[row + 1] - heights[row - 1]) * 0.5
                new_east = (
                    east
                    - time_step * (gravity * east_west(heights[row]) + east * east_west(east) + north * east_slope)
                    + coriolis * north
                )
                new_north = (
                    north
                    - time_step * (gravity * height_slope + east * east_west(north) + north * north_slope)
                    - coriolis * east
                )
                dst[row, here, :] = heights[row]
                dst[deep + row, here, :] = masked(new_east, row)
                dst[2 * deep + row, here, :] = masked(new_north, row)
                del heights[row - 1]
            src, dst = dst, src

        for f in range(fields):
            for half in range(2):
                lanes = slice(half * LANES, (half + 1) * LANES)
                tiles = [src[f * deep + HALO + row, here, lanes] for row in range(rows)]
                for p, tile in enumerate(block_transpose(tiles)):
                    state_ref[half * 8 + p, here, f * LANES : (f + 1) * LANES] = tile
        return carry

    lax.fori_loop(0, members // GROUP, one_group, 0)

    for p in range(patches):
        window[p] = state_ref[p].astype(jnp.bfloat16)
    cells = fields * LANES
    spot_of = lax.broadcasted_iota(jnp.int32, (cells, index_ref.shape[1]), 0)
    for p in range(patches):
        index = index_ref[p : p + 1, :]
        field_row = (index * 1366) >> 16
        column = index - field_row * (3 * BLOCK)
        part = column >> 4
        spot = field_row * BLOCK + (column & (BLOCK - 1))
        total = None
        for k in range(3):
            wanted = jnp.where(part == k, spot, -1)
            chosen = jnp.where(spot_of == wanted, 1.0, 0.0).astype(jnp.bfloat16)
            piece = jnp.dot(window[(p + k - 1) % patches], chosen, preferred_element_type=jnp.float32)
            total = piece if total is None else total + piece
        observed_ref[p] = total.astype(jnp.bfloat16)


def split(x):
    high = x.astype(jnp.bfloat16)
    return high, (x - high.astype(jnp.float32)).astype(jnp.bfloat16)


def mul3(a, b):
    def dot(x, y):
        return jnp.dot(x, y, preferred_element_type=jnp.float32)

    return dot(a[0], b[0]) + (dot(a[0], b[1]) + dot(a[1], b[0]))


def three_rows(x):
    high = x.astype(jnp.bfloat16).astype(jnp.float32)
    rest = x - high
    middle = rest.astype(jnp.bfloat16).astype(jnp.float32)
    low = rest - middle
    shape = (16, x.shape[1])
    row = lax.broadcasted_iota(jnp.int32, shape, 0)
    stacked = jnp.where(row == 0, high, jnp.where(row == 1, middle, jnp.where(row == 2, low, 0.0)))
    return stacked.astype(jnp.bfloat16)


def weights_kernel(observed_ref, index_ref, values_ref, var_ref, high_ref, low_ref):
    members = observed_ref.shape[0]
    wide = observed_ref[...].astype(jnp.float32)
    obs_mean = jnp.sum(wide, axis=0, keepdims=True) * (1.0 / members)
    perturb = (wide - obs_mean).astype(jnp.bfloat16)
    index = index_ref[...]
    column = (index - ((index * 1366) >> 16) * (3 * BLOCK)).astype(jnp.float32)
    taper = jnp.exp(-0.5 * jnp.square((column - (3 * BLOCK - 1) * 0.5) / BLOCK))
    obs_weight = taper / var_ref[...]
    weighted = (perturb.astype(jnp.float32) * obs_weight).astype(jnp.bfloat16)
    contract = (((1,), (1,)), ((), ()))
    gram = lax.dot_general(perturb, weighted, contract, preferred_element_type=jnp.float32)
    row = lax.broadcasted_iota(jnp.int32, (members, members), 0)
    col = lax.broadcasted_iota(jnp.int32, (members, members), 1)
    unit = jnp.where(row == col, 1.0, 0.0)
    system = (members - 1) * unit + gram
    norm_bound = jnp.max(jnp.sum(jnp.abs(system), axis=0, keepdims=True), axis=1, keepdims=True)
    iterate = system / norm_bound
    middle = 1.5 * unit - 0.5 * iterate
    inverse_parts = split(middle)
    iterate_parts = split(mul3(split(iterate), inverse_parts))
    inverse = None
    for turn in range(1, NEWTON):
        middle_parts = split(1.5 * unit - 0.5 * mul3(inverse_parts, iterate_parts))
        inverse = mul3(middle_parts, inverse_parts)
        inverse_parts = split(inverse)
        if turn + 1 < NEWTON:
            iterate_parts = split(mul3(iterate_parts, middle_parts))

    def through(x):
        rows = three_rows(x)
        both = jnp.dot(rows, inverse_parts[0], preferred_element_type=jnp.float32) + jnp.dot(
            rows, inverse_parts[1], preferred_element_type=jnp.float32
        )
        return jnp.sum(both, axis=0, keepdims=True)

    innovation = obs_weight * (values_ref[...] - obs_mean)
    pulled = jnp.sum(
        lax.dot_general(three_rows(innovation), perturb, contract, preferred_element_type=jnp.float32),
        axis=0,
        keepdims=True,
    )
    mean_weight = through(through(pulled)) / norm_bound
    weights = (math.sqrt(members - 1) * lax.rsqrt(norm_bound)) * inverse + mean_weight
    high_ref[...], low_ref[...] = split(weights)


def update_kernel(state_ref, high_ref, low_ref, out_ref):
    state = state_ref[...]
    state_mean = jnp.sum(state, axis=0, keepdims=True) * (1.0 / state.shape[0])
    spread = split(state - state_mean)
    out_ref[...] = state_mean + mul3((high_ref[...], low_ref[...]), spread)


def unpack_kernel(returned_ref, out_ref):
    fields, rows = 3, 8
    stride = fields * rows * 2
    for f in range(fields):
        for half in range(2):
            tiles = [returned_ref[half * 8 + p, :, f * LANES : (f + 1) * LANES] for p in range(8)]
            for r, tile in enumerate(block_transpose(tiles)):
                out_ref[pl.ds(f * 2 * rows + half * rows + r, GROUP, stride=stride), :] = tile


def body(prior_collection, obs_index, obs_values, obs_var):
    members_here, fields, rows, cols = prior_collection.shape
    bands = lax.axis_size("band")
    patches = lax.axis_size("mem")
    members = members_here * patches
    nobs = obs_index.shape[-1]
    cells = fields * rows * BLOCK
    f32, bf16 = jnp.float32, jnp.bfloat16
    shaped = jax.ShapeDtypeStruct
    prior = tiled_view(prior_collection)

    halo_shape = (fields * HALO, members_here, cols)
    first, last = pl.pallas_call(
        edges_kernel, out_shape=(shaped(halo_shape, bf16), shaped(halo_shape, bf16)), name="edges"
    )(prior)
    up = [(i, i + 1) for i in range(bands - 1)]
    down = [(j, i) for i, j in up]
    above = lax.ppermute(last, "band", up)
    below = lax.ppermute(first, "band", down)

    band = lax.axis_index("band")
    inside = jnp.stack([band > 0, band < bands - 1]).astype(f32)
    vmem = pl.BlockSpec(memory_space=pltpu.VMEM)
    smem = pl.BlockSpec(memory_space=pltpu.SMEM)
    deep = (fields * (rows + 2 * HALO), members_here, cols)
    state, observed = pl.pallas_call(
        forecast_kernel,
        in_specs=[smem, vmem, vmem, vmem, vmem],
        out_shape=(shaped((patches, members_here, cells), f32), shaped((patches, members_here, nobs), bf16)),
        scratch_shapes=[
            pltpu.VMEM(deep, f32),
            pltpu.VMEM(deep, f32),
            pltpu.VMEM((patches, members_here, cells), bf16),
        ],
        name="forecast",
    )(inside, prior, above, below, obs_index[0])

    observed = lax.all_to_all(observed, "mem", 0, 0, tiled=True).reshape(members, nobs)
    state = lax.all_to_all(state.astype(jnp.float16), "mem", 0, 0, tiled=True)
    own_index = lax.dynamic_index_in_dim(obs_index[0], lax.axis_index("mem"), 0, keepdims=True)
    high, low = pl.pallas_call(
        weights_kernel,
        out_shape=(shaped((members, members), bf16), shaped((members, members), bf16)),
        cost_estimate=pl.CostEstimate(flops=2 * 19 * members**3, bytes_accessed=2 * 1024 * 1024, transcendentals=0),
        name="weights",
    )(observed, own_index, obs_values[0], obs_var[0])
    analysed = pl.pallas_call(
        update_kernel, out_shape=shaped((members, cells), f32), name="update"
    )(state.astype(f32).reshape(members, cells), high, low)
    returned = lax.all_to_all(
        analysed.astype(jnp.float16).reshape(patches, members_here, cells), "mem", 0, 0, tiled=True
    )
    per_group = GROUP * fields * rows * cols // LANES
    out = pl.pallas_call(
        unpack_kernel,
        grid=(members_here // GROUP,),
        in_specs=[pl.BlockSpec((patches, GROUP, cells), lambda g: (0, g, 0))],
        out_specs=pl.BlockSpec((per_group, LANES), lambda g: (g, 0)),
        out_shape=shaped((members_here * fields * rows * cols // LANES, LANES), f32),
        name="unpack",
    )(returned.astype(f32))
    return untiled_view(out, prior_collection.shape)


def solution(mesh):
    in_specs = (
        P("mem", None, "band", None),
        P("band", None, None),
        P("band", "mem", None),
        P("band", "mem", None),
    )
    out_specs = P("mem", None, "band", None)
    return jax.shard_map(body, mesh=mesh, in_specs=in_specs, out_specs=out_specs, check_vma=False)
```

profile of v0, /device:TPU:2, one launch (start us, length us, event | category | flops | bytes accessed | tf_op | source)
XLA Modules:
  0.0 116.5 jit_solution(7964636274641711586)
XLA Ops:
  0.0 2.2 %edges.1 = (bf16[18,32,256]{2,1,0:T(8,128)(2,1)}, bf16[18,32,256]{2,1,0:T(8,128)(2,1)}) custom-call(f32[1536,128]{1,0:T(8,128)} %bitcast.22), custom_call_target="tpu_custom_call" | custom-call | tf_op jit(solution)/shard_map/edges/pallas_call | solution.py:283
  2.2 1.9 %collective-permute-start = (bf16[18,32,256]{2,1,0:T(8,128)(2,1)}, bf16[18,32,256]{2,1,0:T(8,128)(2,1)S(1)}, u32[]{:S(2)}, u32[]{:S(2)}) collective-permute-start(bf16[18,32,256]{2,1,0:T(8,128)(2,1)} %get-tuple-element.11), channel_id=1, source_target_pairs={{0,1},{1,2},{2,3},{3,4},{4,5},{5,6},{6,7},{7,8},{8,9},{9,10},{10,1... | collective-permute-start | bytes 884744 | tf_op jit(solution)/shard_map/ppermute | solution.py:288
  4.1 16.7 %collective-permute-start.1 = (bf16[18,32,256]{2,1,0:T(8,128)(2,1)}, bf16[18,32,256]{2,1,0:T(8,128)(2,1)S(1)}, u32[]{:S(2)}, u32[]{:S(2)}) collective-permute-start(bf16[18,32,256]{2,1,0:T(8,128)(2,1)} %get-tuple-element.12), channel_id=1, source_target_pairs={{1,0},{2,1},{3,2},{4,3},{5,4},{6,5},{7,6},{8,7},{9,8},{10,9},{11,1... | collective-permute-start | bytes 884744 | tf_op jit(solution)/shard_map/ppermute | solution.py:289
  20.9 0.7 add_convert_fusion.inside_ref
  21.5 2.0 %collective-permute-done.above_ref = bf16[18,32,256]{2,1,0:T(8,128)(2,1)S(1)} collective-permute-done((bf16[18,32,256]{2,1,0:T(8,128)(2,1)}, bf16[18,32,256]{2,1,0:T(8,128)(2,1)S(1)}, u32[]{:S(2)}, u32[]{:S(2)}) %collective-permute-start) | collective-permute-done | bytes 294944 | tf_op jit(solution)/shard_map/ppermute | solution.py:288
  23.5 0.0 copy-start
  23.5 1.9 %collective-permute-done.1.below_ref = bf16[18,32,256]{2,1,0:T(8,128)(2,1)S(1)} collective-permute-done((bf16[18,32,256]{2,1,0:T(8,128)(2,1)}, bf16[18,32,256]{2,1,0:T(8,128)(2,1)S(1)}, u32[]{:S(2)}, u32[]{:S(2)}) %collective-permute-start.1) | collective-permute-done | bytes 294944 | tf_op jit(solution)/shard_map/ppermute | solution.py:289
  25.4 0.0 copy-start.1
  25.4 0.0 copy-done
  25.4 0.7 copy-done.1
  26.1 12.4 %forecast.1 = (f32[16,32,384]{2,1,0:T(8,128)}, bf16[16,32,256]{2,1,0:T(8,128)(2,1)}) custom-call(f32[2]{0:T(128)} %add_convert_fusion.inside_ref, f32[1536,128]{1,0:T(8,128)} %bitcast.23, bf16[18,32,256]{2,1,0:T(8,128)(2,1)} %copy-done, bf16[18,32,256]{2,1,0:T(8,128)(2,1)} %copy-done.1, s32[16,256]{1,0:T(8,128)} %bitcast.26), custom_call_target="tpu_custom_call" | custom-call | tf_op jit(solution)/shard_map/forecast/pallas_call | solution.py:296
  38.5 12.6 %all-to-all-start.1 = ((bf16[16,32,256]{2,1,0:T(8,128)(2,1)}), bf16[16,32,256]{2,1,0:T(8,128)(2,1)S(1)}, u32[]{:S(2)}, u32[]{:S(2)}) async-start(bf16[16,32,256]{2,1,0:T(8,128)(2,1)} %get-tuple-element.14), calls=%async_computation.1 | async-start | bytes 524288 | tf_op jit(solution)/shard_map/all_to_all | solution.py:308
  51.1 1.9 %convert_element_type.14 = f16[16,32,384]{2,1,0:T(8,128)(2,1)} convert(f32[16,32,384]{2,1,0:T(8,128)} %get-tuple-element.13) | non-fusion elementwise | flops 196608 | bytes 1179648 | tf_op jit(solution)/shard_map/convert_element_type | solution.py:309
  53.0 12.1 %all-to-all-done.1 = bf16[16,32,256]{2,1,0:T(8,128)(2,1)S(1)} async-done(((bf16[16,32,256]{2,1,0:T(8,128)(2,1)}), bf16[16,32,256]{2,1,0:T(8,128)(2,1)S(1)}, u32[]{:S(2)}, u32[]{:S(2)}) %all-to-all-start.1) | async-done | bytes 262176 | tf_op jit(solution)/shard_map/all_to_all | solution.py:308
  65.2 0.0 copy-start.2
  65.2 0.7 copy-done.2
  65.9 3.6 %all-to-all-start = ((f16[16,32,384]{2,1,0:T(8,128)(2,1)}), f16[16,32,384]{2,1,0:T(8,128)(2,1)S(1)}, u32[]{:S(2)}, u32[]{:S(2)}) async-start(f16[16,32,384]{2,1,0:T(8,128)(2,1)} %convert_element_type.14), calls=%async_computation | async-start | bytes 786432 | tf_op jit(solution)/shard_map/all_to_all | solution.py:309
  69.4 1.3 %dynamic-slice_bitcast_fusion.index_ref = s32[1,256]{1,0:T(1,128)} fusion(s32[1,16,256]{2,1,0:T(8,128)} %param.5, s32[]{:T(128)S(6)} %select_n.4), kind=kLoop, calls=%fused_computation.2 | loop fusion | bytes 2052 | tf_op jit(solution)/shard_map/jit(dynamic_index_in_dim)/dynamic_slice | solution.py:310
  70.7 8.6 %weights.1 = (bf16[512,512]{1,0:T(8,128)(2,1)}, bf16[512,512]{1,0:T(8,128)(2,1)}) custom-call(bf16[512,256]{1,0:T(8,128)(2,1)} %bitcast.25, s32[1,256]{1,0:T(1,128)} %dynamic-slice_bitcast_fusion.index_ref, f32[1,256]{1,0:T(1,128)} %bitcast.27, f32[1,256]{1,0:T(1,128)} %bitcast.28), custom_call_target="tpu_custom_call" | custom-call | flops 5100273664 | bytes 2097152 | tf_op jit(solution)/shard_map/weights/pallas_call | solution.py:311
  79.3 5.2 %all-to-all-done = f16[16,32,384]{2,1,0:T(8,128)(2,1)S(1)} async-done(((f16[16,32,384]{2,1,0:T(8,128)(2,1)}), f16[16,32,384]{2,1,0:T(8,128)(2,1)S(1)}, u32[]{:S(2)}, u32[]{:S(2)}) %all-to-all-start) | async-done | bytes 393248 | tf_op jit(solution)/shard_map/all_to_all | solution.py:309
  84.5 1.0 bitcast_convert_fusion.state_ref
  85.5 3.4 %update.1 = f32[512,384]{1,0:T(8,128)} custom-call(f32[512,384]{1,0:T(8,128)} %bitcast_convert_fusion.state_ref, bf16[512,512]{1,0:T(8,128)(2,1)} %get-tuple-element.15.high_ref, bf16[512,512]{1,0:T(8,128)(2,1)} %get-tuple-element.16.low_ref), custom_call_target="tpu_custom_call" | custom-call | tf_op jit(solution)/shard_map/update/pallas_call | solution.py:317
  88.8 1.2 %convert_element_type.15 = f16[512,384]{1,0:T(8,128)(2,1)S(1)} convert(f32[512,384]{1,0:T(8,128)} %update.1) | non-fusion elementwise | flops 196608 | bytes 1179648 | tf_op jit(solution)/shard_map/convert_element_type | solution.py:321
  90.0 21.7 %all_to_all.15 = f16[16,32,384]{2,1,0:T(8,128)(2,1)S(1)} all-to-all(f16[16,32,384]{2,1,0:T(8,128)(2,1)S(1)} %bitcast.24), channel_id=1, replica_groups=mesh['mem'=16,'band'=64] {'mem'}, dimensions={0} | all-to-all | bytes 786432 | tf_op jit(solution)/shard_map/all_to_all | solution.py:320
  111.8 1.0 convert_element_type.16.returned_ref
  112.7 3.7 %unpack.1 = f32[1536,128]{1,0:T(8,128)} custom-call(f32[16,32,384]{2,1,0:T(8,128)} %convert_element_type.16.returned_ref), custom_call_target="tpu_custom_call" | custom-call | tf_op jit(solution)/shard_map/unpack/pallas_call | solution.py:324
Async XLA Ops:
  2.2 21.3 %collective-permute-start = (bf16[18,32,256]{2,1,0:T(8,128)(2,1)}, bf16[18,32,256]{2,1,0:T(8,128)(2,1)S(1)}, u32[]{:S(2)}, u32[]{:S(2)}) collective-permute-start(bf16[18,32,256]{2,1,0:T(8,128)(2,1)} %get-tuple-element.11), channel_id=1, source_target_pairs={{0,1},{1,2},{2,3},{3,4},{4,5},{5,6},{6,7},{7,8},{8,9},{9,10},{10,1... | collective-permute-start | bytes 884744 | tf_op jit(solution)/shard_map/ppermute | solution.py:288
  4.1 21.3 %collective-permute-start.1 = (bf16[18,32,256]{2,1,0:T(8,128)(2,1)}, bf16[18,32,256]{2,1,0:T(8,128)(2,1)S(1)}, u32[]{:S(2)}, u32[]{:S(2)}) collective-permute-start(bf16[18,32,256]{2,1,0:T(8,128)(2,1)} %get-tuple-element.12), channel_id=1, source_target_pairs={{1,0},{2,1},{3,2},{4,3},{5,4},{6,5},{7,6},{8,7},{9,8},{10,9},{11,1... | collective-permute-start | bytes 884744 | tf_op jit(solution)/shard_map/ppermute | solution.py:289
  23.5 1.9 %copy-start = (bf16[18,32,256]{2,1,0:T(8,128)(2,1)}, bf16[18,32,256]{2,1,0:T(8,128)(2,1)S(1)}, u32[]{:S(2)}) copy-start(bf16[18,32,256]{2,1,0:T(8,128)(2,1)S(1)} %collective-permute-done.above_ref) | copy-start | bytes 884740
  25.4 0.7 copy-start.1
  38.5 26.6 %all-to-all-start.1 = ((bf16[16,32,256]{2,1,0:T(8,128)(2,1)}), bf16[16,32,256]{2,1,0:T(8,128)(2,1)S(1)}, u32[]{:S(2)}, u32[]{:S(2)}) async-start(bf16[16,32,256]{2,1,0:T(8,128)(2,1)} %get-tuple-element.14), calls=%async_computation.1 | async-start | bytes 524288 | tf_op jit(solution)/shard_map/all_to_all | solution.py:308
  65.2 0.7 copy-start.2
  65.9 18.6 %all-to-all-start = ((f16[16,32,384]{2,1,0:T(8,128)(2,1)}), f16[16,32,384]{2,1,0:T(8,128)(2,1)S(1)}, u32[]{:S(2)}, u32[]{:S(2)}) async-start(f16[16,32,384]{2,1,0:T(8,128)(2,1)} %convert_element_type.14), calls=%async_computation | async-start | bytes 786432 | tf_op jit(solution)/shard_map/all_to_all | solution.py:309
where the time goes:
time: 117 us; the launch traced here: 116 us
  starting transfers between devices  34.8 us (30%)
  Pallas kernels  30.4 us (26%)
  blocking collectives  21.7 us (19%)
  waiting for transfers between devices  21.2 us (18%)
  other arithmetic  5.73 us (5%)
  local copies, waits for them, and re-layouts  2.7 us (2%)
    all_to_all x1, blocking collectives, body(): lax.all_to_all(analysed.astype(jnp.float16).reshape(patches, members_here...  21.7 us
    ppermute x1, starting transfers between devices, body(): below = lax.ppermute(first, 'band', down)  16.7 us
    all_to_all x1, starting transfers between devices, body(): lax.all_to_all(observed, 'mem', 0, 0, tiled=True).reshape(members, nobs)  12.6 us
    pallas_call x1, Pallas kernels, body(): pl.pallas_call(forecast_kernel, in_specs=[smem, vmem, vmem, vmem, vmem],...  12.4 us
    all_to_all x1, waiting for transfers between devices, body(): lax.all_to_all(observed, 'mem', 0, 0, tiled=True).reshape(members, nobs)  12.1 us
    pallas_call x1, Pallas kernels, body(): pl.pallas_call(weights_kernel, out_shape=(shaped((members, members), bf16...  8.61 us
    all_to_all x1, waiting for transfers between devices, body(): state = lax.all_to_all(state.astype(jnp.float16), 'mem', 0, 0, tiled=True)  5.16 us
    pallas_call x1, Pallas kernels, body(): pl.pallas_call(unpack_kernel, grid=(members_here // GROUP,), in_specs=[pl...  3.75 us
  transfers between devices with their start and end apart: 4, of which 4 were waited for; matrix products, arithmetic and copies ran while one was open for 3% of the time, Pallas kernels for 7%

commit v1 on v0

v1 whole, which is shorter than its diff:
```python
import math

import jax
import jax.numpy as jnp
from jax import lax
from jax.experimental import pallas as pl
from jax.experimental.pallas import tpu as pltpu
from jax.sharding import PartitionSpec as P

STEPS = 3
NEWTON = 3
HALO = 2 * STEPS

time_step = 0.1
gravity = 1.0
coriolis = 0.05
mean_depth = 1.0

GROUP = 8
LANES = 128
BLOCK = 16
PASSES = 1


def tiled_view(x):
    m, f, r, c = x.shape
    halves = c // LANES
    return x.reshape(m, f, r, halves, LANES).transpose(0, 1, 3, 2, 4).reshape(-1, LANES)


def untiled_view(x, shape):
    m, f, r, c = shape
    halves = c // LANES
    return x.reshape(m, f, halves, r, LANES).transpose(0, 1, 3, 2, 4).reshape(shape)


def block_transpose(tiles):
    tiles = list(tiles)
    block = lax.broadcasted_iota(jnp.int32, tiles[0].shape, 1) // BLOCK
    for s in (4, 2, 1):
        high = (block & s) != 0
        for i in range(8):
            if i & s:
                continue
            a, b = tiles[i], tiles[i + s]
            tiles[i] = jnp.where(high, pltpu.roll(b, BLOCK * s, 1), a)
            tiles[i + s] = jnp.where(high, b, pltpu.roll(a, LANES - BLOCK * s, 1))
    return tiles


def edges_kernel(prior_ref, first_ref, last_ref):
    fields, rows = 3, 8
    stride = fields * rows * 2
    for member in range(0, first_ref.shape[1], 2 * GROUP):
        for f in range(fields):
            for half in range(2):
                lanes = slice(half * LANES, (half + 1) * LANES)
                for row in range(rows):
                    parts = [
                        prior_ref[pl.ds((m * fields + f) * 2 * rows + half * rows + row, GROUP, stride=stride), :]
                        for m in (member, member + GROUP)
                    ]
                    both = jnp.concatenate(parts, axis=0).astype(jnp.bfloat16)
                    if row < HALO:
                        first_ref[f * HALO + row, member : member + 2 * GROUP, lanes] = both
                    if row >= rows - HALO:
                        last_ref[f * HALO + row - (rows - HALO), member : member + 2 * GROUP, lanes] = both


def east_west(x):
    cols = x.shape[-1]
    return pltpu.roll(x, cols - 1, 1) - pltpu.roll(x, 1, 1)


def forecast_kernel(inside_ref, prior_ref, above_ref, below_ref, index_ref, exact_ref, sent_ref, ping, pong):
    fields, rows = 3, 8
    deep = rows + 2 * HALO
    stride = fields * rows * 2
    patches = sent_ref.shape[0]
    cells = fields * LANES
    above_in = inside_ref[0]
    below_in = inside_ref[1]
    half_step = 0.5 * time_step

    for f in range(fields):
        for row in range(HALO):
            ping[f * deep + row] = above_ref[f * HALO + row].astype(jnp.float32)
            ping[f * deep + HALO + rows + row] = below_ref[f * HALO + row].astype(jnp.float32)
        for half in range(2):
            for row in range(rows):
                start = f * 2 * rows + half * rows + row
                ping[f * deep + HALO + row, :, half * LANES : (half + 1) * LANES] = prior_ref[
                    pl.ds(start, GROUP, stride=stride), :
                ]

    def masked(x, row):
        if row < HALO:
            return x * above_in
        if row >= HALO + rows:
            return x * below_in
        return x

    src, dst = ping, pong
    for turn in range(STEPS):
        low = 2 * (turn + 1)
        high = deep - 2 * (turn + 1)
        north_flux = {}

        def flux(row):
            if row not in north_flux:
                north_flux[row] = (mean_depth + src[row]) * src[2 * deep + row]
            return north_flux[row]

        def new_height(row):
            height = src[row]
            flux_east = (mean_depth + height) * src[deep + row]
            return masked(height - half_step * (east_west(flux_east) + (flux(row + 1) - flux(row - 1))), row)

        heights = {row: new_height(row) for row in (low - 1, low)}
        for row in range(low, high):
            heights[row + 1] = new_height(row + 1)
            east = src[deep + row]
            north = src[2 * deep + row]
            east_slope = src[deep + row + 1] - src[deep + row - 1]
            north_slope = src[2 * deep + row + 1] - src[2 * deep + row - 1]
            height_slope = heights[row + 1] - heights[row - 1]
            new_east = (
                east
                - half_step * (gravity * east_west(heights[row]) + east * east_west(east) + north * east_slope)
                + coriolis * north
            )
            new_north = (
                north
                - half_step * (gravity * height_slope + east * east_west(north) + north * north_slope)
                - coriolis * east
            )
            dst[row] = heights[row]
            dst[deep + row] = masked(new_east, row)
            dst[2 * deep + row] = masked(new_north, row)
            del heights[row - 1]
        src, dst = dst, src

    for f in range(fields):
        for half in range(2):
            lanes = slice(half * LANES, (half + 1) * LANES)
            tiles = [src[f * deep + HALO + row, :, lanes] for row in range(rows)]
            for p, tile in enumerate(block_transpose(tiles)):
                exact_ref[half * 8 + p, :, f * LANES : (f + 1) * LANES] = tile
    for p in range(patches):
        sent_ref[p, :, :cells] = exact_ref[p].astype(jnp.bfloat16)

    index = index_ref[...]
    field_row = (index * 1366) >> 16
    column = index - field_row * (3 * BLOCK)
    tile_of = (column >> 4) * fields + (field_row >> 3)
    lane_of = (field_row & 7) * BLOCK + (column & (BLOCK - 1))
    for p in range(patches):
        for half in range(index.shape[1] // LANES):
            lanes = slice(half * LANES, (half + 1) * LANES)
            tile = jnp.broadcast_to(tile_of[p : p + 1, lanes], (GROUP, LANES))
            lane = jnp.broadcast_to(lane_of[p : p + 1, lanes], (GROUP, LANES))
            picked = None
            for k in range(3):
                for f in range(fields):
                    values = exact_ref[(p + k - 1) % patches, :, f * LANES : (f + 1) * LANES]
                    values = jnp.take_along_axis(values, lane, axis=1, mode="promise_in_bounds")
                    picked = values if picked is None else jnp.where(tile == k * fields + f, values, picked)
            sent_ref[p, :, cells + half * LANES : cells + (half + 1) * LANES] = picked.astype(jnp.bfloat16)


def split(x):
    high = x.astype(jnp.bfloat16)
    return high, (x - high.astype(jnp.float32)).astype(jnp.bfloat16)


def mul3(a, b):
    def dot(x, y):
        return jnp.dot(x, y, preferred_element_type=jnp.float32)

    return dot(a[0], b[0]) + (dot(a[0], b[1]) + dot(a[1], b[0]))


def three_rows(x):
    high = x.astype(jnp.bfloat16).astype(jnp.float32)
    rest = x - high
    middle = rest.astype(jnp.bfloat16).astype(jnp.float32)
    low = rest - middle
    shape = (16, x.shape[1])
    row = lax.broadcasted_iota(jnp.int32, shape, 0)
    stacked = jnp.where(row == 0, high, jnp.where(row == 1, middle, jnp.where(row == 2, low, 0.0)))
    return stacked.astype(jnp.bfloat16)


def analyse_kernel(here_ref, got_ref, index_ref, values_ref, var_ref, out_ref):
    members = got_ref.shape[0]
    cells = got_ref.shape[1] - values_ref.shape[1]
    wide = got_ref[:, cells:].astype(jnp.float32)
    obs_mean = jnp.sum(wide, axis=0, keepdims=True) * (1.0 / members)
    perturb = (wide - obs_mean).astype(jnp.bfloat16)
    index = index_ref[pl.ds(here_ref[0], 1), :]
    column = (index - ((index * 1366) >> 16) * (3 * BLOCK)).astype(jnp.float32)
    taper = jnp.exp(-0.5 * jnp.square((column - (3 * BLOCK - 1) * 0.5) / BLOCK))
    obs_weight = taper / var_ref[...]
    weighted = (perturb.astype(jnp.float32) * obs_weight).astype(jnp.bfloat16)
    contract = (((1,), (1,)), ((), ()))
    gram = lax.dot_general(perturb, weighted, contract, preferred_element_type=jnp.float32)
    row = lax.broadcasted_iota(jnp.int32, (members, members), 0)
    col = lax.broadcasted_iota(jnp.int32, (members, members), 1)
    on_diagonal = row == col
    lengths = jnp.sum(jnp.abs(gram), axis=0, keepdims=True)
    diagonal = jnp.sum(jnp.where(on_diagonal, gram, 0.0), axis=0, keepdims=True)
    lengths = lengths + (jnp.abs(diagonal + (members - 1)) - jnp.abs(diagonal))
    norm_bound = jnp.max(lengths, axis=1, keepdims=True)

    def mul(a, b):
        if PASSES == 3:
            rest = mul3(split(a[1]), split(b[1]))
        else:
            rest = jnp.dot(
                a[1].astype(jnp.bfloat16), b[1].astype(jnp.bfloat16), preferred_element_type=jnp.float32
            )
        return a[0] * b[0], a[0] * b[1] + b[0] * a[1] + rest

    def middle_of(a):
        return 1.5 - 0.5 * a[0], -0.5 * a[1]

    inverse_bound = 1.0 / norm_bound
    iterate = ((members - 1) * inverse_bound, gram * inverse_bound)
    middle = middle_of(iterate)
    inverse = middle
    for turn in range(1, NEWTON):
        iterate = mul(iterate, middle)
        middle = middle_of(mul(inverse, iterate))
        inverse = mul(middle, inverse)
    scale, rest = inverse
    rest_parts = split(rest)

    def through(x):
        rows = three_rows(x)
        both = jnp.dot(rows, rest_parts[0], preferred_element_type=jnp.float32) + jnp.dot(
            rows, rest_parts[1], preferred_element_type=jnp.float32
        )
        return scale * x + jnp.sum(both, axis=0, keepdims=True)

    innovation = obs_weight * (values_ref[...] - obs_mean)
    pulled = jnp.sum(
        lax.dot_general(three_rows(innovation), perturb, contract, preferred_element_type=jnp.float32),
        axis=0,
        keepdims=True,
    )
    mean_weight = through(through(pulled)) * inverse_bound
    grow = math.sqrt(members - 1) * lax.rsqrt(norm_bound)
    diagonal = jnp.sum(jnp.where(on_diagonal, rest, 0.0), axis=0, keepdims=True)
    average = jnp.sum(diagonal, axis=1, keepdims=True) * (1.0 / members)
    kept = (grow * (scale + average)).astype(jnp.bfloat16).astype(jnp.float32)
    change = grow * rest + mean_weight + jnp.where(on_diagonal, grow * scale - kept, 0.0)
    change = change.astype(jnp.bfloat16)

    fields = cells // LANES
    patches, here = out_ref.shape[0], members // out_ref.shape[0]
    state = got_ref[:, :cells].astype(jnp.float32)
    state_mean = jnp.sum(state, axis=0, keepdims=True) * (1.0 / members)
    high, low = split(state - state_mean)
    moved = (1.0 - kept) * state_mean + (
        jnp.dot(change, high, preferred_element_type=jnp.float32)
        + jnp.dot(change, low, preferred_element_type=jnp.float32)
    )
    kept_rows = jnp.broadcast_to(kept, (8, LANES)).astype(jnp.bfloat16)
    for p in range(patches):
        for f in range(fields):
            out_ref[p, f * here : (f + 1) * here, :] = moved[
                p * here : (p + 1) * here, f * LANES : (f + 1) * LANES
            ].astype(jnp.bfloat16)
        out_ref[p, fields * here :, :] = kept_rows


def unpack_kernel(returned_ref, exact_ref, out_ref):
    fields, rows = 3, 8
    stride = fields * rows * 2
    per_group = stride * GROUP
    here = (returned_ref.shape[1] - 8) // fields
    count = exact_ref.shape[1]
    first = pl.multiple_of(pl.program_id(0) * count, count)
    for f in range(fields):
        for half in range(2):
            tiles = []
            for p in range(half * 8, half * 8 + 8):
                moved = returned_ref[p, pl.ds(f * here + first, count), :].astype(jnp.float32)
                kept = returned_ref[p, fields * here : fields * here + 8, :].astype(jnp.float32)[0:1, :]
                tiles.append(moved + kept * exact_ref[p, :, f * LANES : (f + 1) * LANES])
            for r, tile in enumerate(block_transpose(tiles)):
                for g in range(count // GROUP):
                    start = g * per_group + f * 2 * rows + half * rows + r
                    out_ref[pl.ds(start, GROUP, stride=stride), :] = tile[g * GROUP : (g + 1) * GROUP]


def body(prior_collection, obs_index, obs_values, obs_var):
    members_here, fields, rows, cols = prior_collection.shape
    bands = lax.axis_size("band")
    patches = lax.axis_size("mem")
    members = members_here * patches
    nobs = obs_index.shape[-1]
    cells = fields * rows * BLOCK
    f32, bf16 = jnp.float32, jnp.bfloat16
    shaped = jax.ShapeDtypeStruct
    prior = tiled_view(prior_collection)

    halo_shape = (fields * HALO, members_here, cols)
    first, last = pl.pallas_call(
        edges_kernel, out_shape=(shaped(halo_shape, bf16), shaped(halo_shape, bf16)), name="edges"
    )(prior)
    up = [(i, i + 1) for i in range(bands - 1)]
    down = [(j, i) for i, j in up]
    above = lax.ppermute(last, "band", up)
    below = lax.ppermute(first, "band", down)

    band = lax.axis_index("band")
    inside = jnp.stack([band > 0, band < bands - 1]).astype(f32)
    vmem = pl.BlockSpec(memory_space=pltpu.VMEM)
    smem = pl.BlockSpec(memory_space=pltpu.SMEM)
    deep = (fields * (rows + 2 * HALO), GROUP, cols)
    groups = members_here // GROUP
    per_group = GROUP * fields * rows * cols // LANES

    def of_group(*shape):
        return pl.BlockSpec(shape, lambda g: (0, g, 0))

    exact, sent = pl.pallas_call(
        forecast_kernel,
        grid=(groups,),
        in_specs=[
            smem,
            pl.BlockSpec((per_group, LANES), lambda g: (g, 0)),
            of_group(fields * HALO, GROUP, cols),
            of_group(fields * HALO, GROUP, cols),
            pl.BlockSpec((patches, nobs), lambda g: (0, 0)),
        ],
        out_specs=[of_group(patches, GROUP, cells), of_group(patches, GROUP, cells + nobs)],
        out_shape=(
            shaped((patches, members_here, cells), f32),
            shaped((patches, members_here, cells + nobs), bf16),
        ),
        scratch_shapes=[pltpu.VMEM(deep, f32), pltpu.VMEM(deep, f32)],
        name="forecast",
    )(inside, prior, above, below, obs_index[0])

    got = lax.all_to_all(sent, "mem", 0, 0, tiled=True).reshape(members, cells + nobs)
    here = lax.axis_index("mem").astype(jnp.int32).reshape(1)
    moved = pl.pallas_call(
        analyse_kernel,
        in_specs=[smem, vmem, vmem, vmem, vmem],
        out_shape=shaped((patches, fields * members_here + 8, LANES), bf16),
        name="analyse",
    )(here, got, obs_index[0], obs_values[0], obs_var[0])
    returned = lax.all_to_all(moved, "mem", 0, 0, tiled=True)
    count = 2 * GROUP
    out = pl.pallas_call(
        unpack_kernel,
        grid=(members_here // count,),
        in_specs=[
            pl.BlockSpec((patches, fields * members_here + 8, LANES), lambda g: (0, 0, 0)),
            pl.BlockSpec((patches, count, cells), lambda g: (0, g, 0)),
        ],
        out_specs=pl.BlockSpec((2 * per_group, LANES), lambda g: (g, 0)),
        out_shape=shaped((members_here * fields * rows * cols // LANES, LANES), f32),
        name="unpack",
    )(returned, exact)
    return untiled_view(out, prior_collection.shape)


def solution(mesh):
    in_specs = (
        P("mem", None, "band", None),
        P("band", None, None),
        P("band", "mem", None),
        P("band", "mem", None),
    )
    out_specs = P("mem", None, "band", None)
    return jax.shard_map(body, mesh=mesh, in_specs=in_specs, out_specs=out_specs, check_vma=False)
```

time: 117 us -> 99.2 us (0.85)
  Pallas kernels: 30.4 us -> 24 us
  other arithmetic: 5.73 us -> 0.62 us
  starting transfers between devices: 34.8 us -> 31.2 us
  blocking collectives: 21.7 us -> 19.3 us
    pallas_call x4 -> x3, Pallas kernels: 28.1 us -> 21.7 us  [the longest x1 12.4 us: body(): pl.pallas_call(forecast_kernel, grid=(groups,), in_specs=[smem, pl.BlockS...]
    convert_element_type x3 -> x0, other arithmetic: 4.1 us -> none  [the longest x1 1.94 us: body(): state = lax.all_to_all(state.astype(jnp.float16), 'mem', 0, 0, tiled=True)]
    all_to_all x2 -> x1, starting transfers between devices: 16.1 us -> 12.6 us  [body(): lax.all_to_all(sent, 'mem', 0, 0, tiled=True).reshape(members, cells + nobs)]
    all_to_all x1, blocking collectives: 21.7 us -> 19.3 us  [body(): returned = lax.all_to_all(moved, 'mem', 0, 0, tiled=True)]
    dynamic_slice x1 -> x0, local copies, waits for them, and re-layouts: 1.28 us -> none  [body(): lax.dynamic_index_in_dim(obs_index[0], lax.axis_index('mem'), 0, keepdims...]
    all_to_all x2 -> x1, waiting for transfers between devices: 17.3 us -> 18.1 us  [body(): lax.all_to_all(sent, 'mem', 0, 0, tiled=True).reshape(members, cells + nobs)]
  transfers between devices with their start and end apart: 4 -> 3, of which waited for: 4 -> 3; matrix products, arithmetic and copies ran while one was open for 3% -> 1% of each run, Pallas kernels for 7% -> 0%
where the time goes in v1:
time: 99.2 us; the launch traced here: 98.7 us
  starting transfers between devices  31.2 us (31%)
  Pallas kernels  24 us (24%)
  waiting for transfers between devices  22 us (22%)
  blocking collectives  19.3 us (19%)
  local copies, waits for them, and re-layouts  1.58 us (2%)
    all_to_all x1, blocking collectives, body(): returned = lax.all_to_all(moved, 'mem', 0, 0, tiled=True)  19.3 us
    all_to_all x1, waiting for transfers between devices, body(): lax.all_to_all(sent, 'mem', 0, 0, tiled=True).reshape(members, cells + nobs)  18.1 us
    ppermute x1, starting transfers between devices, body(): below = lax.ppermute(first, 'band', down)  16.7 us
    all_to_all x1, starting transfers between devices, body(): lax.all_to_all(sent, 'mem', 0, 0, tiled=True).reshape(members, cells + nobs)  12.6 us
    pallas_call x1, Pallas kernels, body(): pl.pallas_call(forecast_kernel, grid=(groups,), in_specs=[smem, pl.BlockS...  12.4 us
    pallas_call x1, Pallas kernels, body(): pl.pallas_call(analyse_kernel, in_specs=[smem, vmem, vmem, vmem, vmem], o...  6.08 us
    pallas_call x1, Pallas kernels, body(): pl.pallas_call(unpack_kernel, grid=(members_here // count,), in_specs=[pl...  3.27 us
    pallas_call x1, Pallas kernels, body(): pl.pallas_call(edges_kernel, out_shape=(shaped(halo_shape, bf16), shaped(...  2.23 us
  transfers between devices with their start and end apart: 3, of which 3 were waited for; matrix products, arithmetic and copies ran while one was open for 1% of the time, Pallas kernels for 0%

profile of v1, /device:TPU:2, one launch (start us, length us, event | category | flops | bytes accessed | tf_op | source)
XLA Modules:
  0.0 98.7 jit_solution(14752006949665486733)
XLA Ops:
  0.0 2.2 %edges.1 = (bf16[18,32,256]{2,1,0:T(8,128)(2,1)}, bf16[18,32,256]{2,1,0:T(8,128)(2,1)}) custom-call(f32[1536,128]{1,0:T(8,128)} %bitcast.17), custom_call_target="tpu_custom_call" | custom-call | tf_op jit(solution)/shard_map/edges/pallas_call | solution.py:309
  2.2 1.9 %collective-permute-start = (bf16[18,32,256]{2,1,0:T(8,128)(2,1)}, bf16[18,32,256]{2,1,0:T(8,128)(2,1)S(1)}, u32[]{:S(2)}, u32[]{:S(2)}) collective-permute-start(bf16[18,32,256]{2,1,0:T(8,128)(2,1)} %get-tuple-element.9), channel_id=1, source_target_pairs={{0,1},{1,2},{2,3},{3,4},{4,5},{5,6},{6,7},{7,8},{8,9},{9,10},{10,1... | collective-permute-start | bytes 884744 | tf_op jit(solution)/shard_map/ppermute | solution.py:314
  4.1 16.7 %collective-permute-start.1 = (bf16[18,32,256]{2,1,0:T(8,128)(2,1)}, bf16[18,32,256]{2,1,0:T(8,128)(2,1)S(1)}, u32[]{:S(2)}, u32[]{:S(2)}) collective-permute-start(bf16[18,32,256]{2,1,0:T(8,128)(2,1)} %get-tuple-element.10), channel_id=1, source_target_pairs={{1,0},{2,1},{3,2},{4,3},{5,4},{6,5},{7,6},{8,7},{9,8},{10,9},{11,1... | collective-permute-start | bytes 884744 | tf_op jit(solution)/shard_map/ppermute | solution.py:315
  20.9 0.6 add_convert_fusion.inside_ref
  21.5 2.0 %collective-permute-done.above_ref = bf16[18,32,256]{2,1,0:T(8,128)(2,1)S(1)} collective-permute-done((bf16[18,32,256]{2,1,0:T(8,128)(2,1)}, bf16[18,32,256]{2,1,0:T(8,128)(2,1)S(1)}, u32[]{:S(2)}, u32[]{:S(2)}) %collective-permute-start) | collective-permute-done | bytes 294944 | tf_op jit(solution)/shard_map/ppermute | solution.py:314
  23.6 0.0 copy-start.1
  23.6 1.9 %collective-permute-done.1.below_ref = bf16[18,32,256]{2,1,0:T(8,128)(2,1)S(1)} collective-permute-done((bf16[18,32,256]{2,1,0:T(8,128)(2,1)}, bf16[18,32,256]{2,1,0:T(8,128)(2,1)S(1)}, u32[]{:S(2)}, u32[]{:S(2)}) %collective-permute-start.1) | collective-permute-done | bytes 294944 | tf_op jit(solution)/shard_map/ppermute | solution.py:315
  25.4 0.0 copy-start.2
  25.4 0.0 copy-done.1
  25.4 0.7 copy-done.2
  26.2 12.4 %forecast.1 = (f32[16,32,384]{2,1,0:T(8,128)}, bf16[16,32,640]{2,1,0:T(8,128)(2,1)}) custom-call(f32[2]{0:T(128)} %add_convert_fusion.inside_ref, f32[1536,128]{1,0:T(8,128)} %bitcast.18, bf16[18,32,256]{2,1,0:T(8,128)(2,1)} %copy-done.1, bf16[18,32,256]{2,1,0:T(8,128)(2,1)} %copy-done.2, s32[16,256]{1,0:T(8,128)} %bitcast.20), custom_call_target="tpu_custom_call" | custom-call | tf_op jit(solution)/shard_map/forecast/pallas_call | solution.py:328
  38.5 12.6 %all-to-all-start = ((bf16[16,32,640]{2,1,0:T(8,128)(2,1)}), bf16[16,32,640]{2,1,0:T(8,128)(2,1)S(1)}, u32[]{:S(2)}, u32[]{:S(2)}) async-start(bf16[16,32,640]{2,1,0:T(8,128)(2,1)} %get-tuple-element.11), calls=%async_computation | async-start | bytes 1310720 | tf_op jit(solution)/shard_map/all_to_all | solution.py:347
  51.1 18.1 %all-to-all-done = bf16[16,32,640]{2,1,0:T(8,128)(2,1)S(1)} async-done(((bf16[16,32,640]{2,1,0:T(8,128)(2,1)}), bf16[16,32,640]{2,1,0:T(8,128)(2,1)S(1)}, u32[]{:S(2)}, u32[]{:S(2)}) %all-to-all-start) | async-done | bytes 655392 | tf_op jit(solution)/shard_map/all_to_all | solution.py:347
  69.2 0.0 copy-start
  69.2 0.8 copy-done
  70.1 6.1 %analyse.1 = bf16[16,104,128]{2,1,0:T(8,128)(2,1)} custom-call(s32[1]{0:T(128)} %bitcast.here_ref, bf16[512,640]{1,0:T(8,128)(2,1)} %bitcast.19, s32[16,256]{1,0:T(8,128)} %bitcast.21, f32[1,256]{1,0:T(1,128)} %bitcast.22, f32[1,256]{1,0:T(1,128)} %bitcast.23), custom_call_target="tpu_custom_call" | custom-call | tf_op jit(solution)/shard_map/analyse/pallas_call | solution.py:349
  76.1 19.3 %all_to_all.10.returned_ref = bf16[16,104,128]{2,1,0:T(8,128)(2,1)} all-to-all(bf16[16,104,128]{2,1,0:T(8,128)(2,1)} %analyse.1), channel_id=1, replica_groups=mesh['mem'=16,'band'=64] {'mem'}, dimensions={0} | all-to-all | bytes 851968 | tf_op jit(solution)/shard_map/all_to_all | solution.py:355
  95.5 3.3 %unpack.1 = f32[1536,128]{1,0:T(8,128)} custom-call(bf16[16,104,128]{2,1,0:T(8,128)(2,1)} %all_to_all.10.returned_ref, f32[16,32,384]{2,1,0:T(8,128)} %get-tuple-element.12.exact_ref), custom_call_target="tpu_custom_call" | custom-call | tf_op jit(solution)/shard_map/unpack/pallas_call | solution.py:357
Async XLA Ops:
  2.2 21.3 %collective-permute-start = (bf16[18,32,256]{2,1,0:T(8,128)(2,1)}, bf16[18,32,256]{2,1,0:T(8,128)(2,1)S(1)}, u32[]{:S(2)}, u32[]{:S(2)}) collective-permute-start(bf16[18,32,256]{2,1,0:T(8,128)(2,1)} %get-tuple-element.9), channel_id=1, source_target_pairs={{0,1},{1,2},{2,3},{3,4},{4,5},{5,6},{6,7},{7,8},{8,9},{9,10},{10,1... | collective-permute-start | bytes 884744 | tf_op jit(solution)/shard_map/ppermute | solution.py:314
  4.1 21.3 %collective-permute-start.1 = (bf16[18,32,256]{2,1,0:T(8,128)(2,1)}, bf16[18,32,256]{2,1,0:T(8,128)(2,1)S(1)}, u32[]{:S(2)}, u32[]{:S(2)}) collective-permute-start(bf16[18,32,256]{2,1,0:T(8,128)(2,1)} %get-tuple-element.10), channel_id=1, source_target_pairs={{1,0},{2,1},{3,2},{4,3},{5,4},{6,5},{7,6},{8,7},{9,8},{10,9},{11,1... | collective-permute-start | bytes 884744 | tf_op jit(solution)/shard_map/ppermute | solution.py:315
  23.6 1.9 %copy-start.1 = (bf16[18,32,256]{2,1,0:T(8,128)(2,1)}, bf16[18,32,256]{2,1,0:T(8,128)(2,1)S(1)}, u32[]{:S(2)}) copy-start(bf16[18,32,256]{2,1,0:T(8,128)(2,1)S(1)} %collective-permute-done.above_ref) | copy-start | bytes 884740
  25.4 0.7 copy-start.2
  38.5 30.7 %all-to-all-start = ((bf16[16,32,640]{2,1,0:T(8,128)(2,1)}), bf16[16,32,640]{2,1,0:T(8,128)(2,1)S(1)}, u32[]{:S(2)}, u32[]{:S(2)}) async-start(bf16[16,32,640]{2,1,0:T(8,128)(2,1)} %get-tuple-element.11), calls=%async_computation | async-start | bytes 1310720 | tf_op jit(solution)/shard_map/all_to_all | solution.py:347
  69.2 0.8 copy-start

commit v2 on v1

--- a/solution.py
+++ b/solution.py
@@ -20,6 +20,14 @@
 LANES = 128
 BLOCK = 16
 PASSES = 1
+
+
+def in_vmem(shape, dtype):
+    return pltpu.VMEM(shape, dtype)
+
+
+def to_vmem(x):
+    return pltpu.with_memory_space_constraint(x, pltpu.VMEM)
 
 
 def tiled_view(x):
@@ -67,31 +75,50 @@
                         last_ref[f * HALO + row - (rows - HALO), member : member + 2 * GROUP, lanes] = both
 
 
+def window_spots(index):
+    field_row = (index * 1366) >> 16
+    column = index - field_row * (3 * BLOCK)
+    return (column >> 4) * (3 * LANES) + field_row * BLOCK + (column & (BLOCK - 1))
+
+
+def stage_kernel(prior_ref, index_ref, own_ref, chosen_ref):
+    fields, rows = 3, 8
+    stride = fields * rows * 2
+    for member in range(0, own_ref.shape[1], GROUP):
+        for f in range(fields):
+            for half in range(2):
+                for row in range(rows):
+                    start = (member * fields + f) * 2 * rows + half * rows + row
+                    own_ref[f * rows + row, member : member + GROUP, half * LANES : (half + 1) * LANES] = prior_ref[
+                        pl.ds(start, GROUP, stride=stride), :
+                    ]
+    spots = window_spots(index_ref[...])
+    order = lax.broadcasted_iota(jnp.int32, chosen_ref.shape[1:], 0)
+    for p in range(chosen_ref.shape[0]):
+        chosen_ref[p] = jnp.where(order == spots[p : p + 1, :], 1.0, 0.0).astype(jnp.bfloat16)
+
+
 def east_west(x):
     cols = x.shape[-1]
     return pltpu.roll(x, cols - 1, 1) - pltpu.roll(x, 1, 1)
 
 
-def forecast_kernel(inside_ref, prior_ref, above_ref, below_ref, index_ref, exact_ref, sent_ref, ping, pong):
+def forecast_kernel(inside_ref, own_ref, above_ref, below_ref, chosen_ref, exact_ref, sent_ref, ping, pong):
     fields, rows = 3, 8
     deep = rows + 2 * HALO
-    stride = fields * rows * 2
     patches = sent_ref.shape[0]
     cells = fields * LANES
     above_in = inside_ref[0]
     below_in = inside_ref[1]
     half_step = 0.5 * time_step
+    here = pl.ds(pl.multiple_of(pl.program_id(0) * GROUP, GROUP), GROUP)
 
     for f in range(fields):
         for row in range(HALO):
-            ping[f * deep + row] = above_ref[f * HALO + row].astype(jnp.float32)
-            ping[f * deep + HALO + rows + row] = below_ref[f * HALO + row].astype(jnp.float32)
-        for half in range(2):
-            for row in range(rows):
-                start = f * 2 * rows + half * rows + row
-                ping[f * deep + HALO + row, :, half * LANES : (half + 1) * LANES] = prior_ref[
-                    pl.ds(start, GROUP, stride=stride), :
-                ]
+            ping[f * deep + row] = above_ref[f * HALO + row, here, :].astype(jnp.float32)
+            ping[f * deep + HALO + rows + row] = below_ref[f * HALO + row, here, :].astype(jnp.float32)
+        for row in range(rows):
+            ping[f * deep + HALO + row] = own_ref[f * rows + row, here, :]
 
     def masked(x, row):
         if row < HALO:
@@ -145,27 +172,22 @@
             lanes = slice(half * LANES, (half + 1) * LANES)
             tiles = [src[f * deep + HALO + row, :, lanes] for row in range(rows)]
             for p, tile in enumerate(block_transpose(tiles)):
-                exact_ref[half * 8 + p, :, f * LANES : (f + 1) * LANES] = tile
+                exact_ref[half * 8 + p, here, f * LANES : (f + 1) * LANES] = tile
     for p in range(patches):
-        sent_ref[p, :, :cells] = exact_ref[p].astype(jnp.bfloat16)
-
-    index = index_ref[...]
-    field_row = (index * 1366) >> 16
-    column = index - field_row * (3 * BLOCK)
-    tile_of = (column >> 4) * fields + (field_row >> 3)
-    lane_of = (field_row & 7) * BLOCK + (column & (BLOCK - 1))
-    for p in range(patches):
-        for half in range(index.shape[1] // LANES):
-            lanes = slice(half * LANES, (half + 1) * LANES)
-            tile = jnp.broadcast_to(tile_of[p : p + 1, lanes], (GROUP, LANES))
-            lane = jnp.broadcast_to(lane_of[p : p + 1, lanes], (GROUP, LANES))
-            picked = None
+        sent_ref[p, here, :cells] = exact_ref[p, here, :].astype(jnp.bfloat16)
+
+    @pl.when(pl.program_id(0) == pl.num_programs(0) - 1)
+    def _():
+        for p in range(patches):
+            total = None
             for k in range(3):
-                for f in range(fields):
-                    values = exact_ref[(p + k - 1) % patches, :, f * LANES : (f + 1) * LANES]
-                    values = jnp.take_along_axis(values, lane, axis=1, mode="promise_in_bounds")
-                    picked = values if picked is None else jnp.where(tile == k * fields + f, values, picked)
-            sent_ref[p, :, cells + half * LANES : cells + (half + 1) * LANES] = picked.astype(jnp.bfloat16)
+                piece = jnp.dot(
+                    sent_ref[(p + k - 1) % patches, :, :cells],
+                    chosen_ref[p, k * cells : (k + 1) * cells, :],
+                    preferred_element_type=jnp.float32,
+                )
+                total = piece if total is None else total + piece
+            sent_ref[p, :, cells:] = total.astype(jnp.bfloat16)
 
 
 def split(x):
@@ -276,10 +298,10 @@
 
 def unpack_kernel(returned_ref, exact_ref, out_ref):
     fields, rows = 3, 8
+    count = 2 * GROUP
     stride = fields * rows * 2
     per_group = stride * GROUP
     here = (returned_ref.shape[1] - 8) // fields
-    count = exact_ref.shape[1]
     first = pl.multiple_of(pl.program_id(0) * count, count)
     for f in range(fields):
         for half in range(2):
@@ -287,7 +309,7 @@
             for p in range(half * 8, half * 8 + 8):
                 moved = returned_ref[p, pl.ds(f * here + first, count), :].astype(jnp.float32)
                 kept = returned_ref[p, fields * here : fields * here + 8, :].astype(jnp.float32)[0:1, :]
-                tiles.append(moved + kept * exact_ref[p, :, f * LANES : (f + 1) * LANES])
+                tiles.append(moved + kept * exact_ref[p, pl.ds(first, count), f * LANES : (f + 1) * LANES])
             for r, tile in enumerate(block_transpose(tiles)):
                 for g in range(count // GROUP):
                     start = g * per_group + f * 2 * rows + half * rows + r
@@ -306,65 +328,79 @@
     prior = tiled_view(prior_collection)
 
     halo_shape = (fields * HALO, members_here, cols)
+    vmem = pl.BlockSpec(memory_space=pltpu.VMEM)
+    smem = pl.BlockSpec(memory_space=pltpu.SMEM)
     first, last = pl.pallas_call(
-        edges_kernel, out_shape=(shaped(halo_shape, bf16), shaped(halo_shape, bf16)), name="edges"
+        edges_kernel,
+        out_specs=[vmem, vmem],
+        out_shape=(in_vmem(halo_shape, bf16), in_vmem(halo_shape, bf16)),
+        name="edges",
     )(prior)
     up = [(i, i + 1) for i in range(bands - 1)]
     down = [(j, i) for i, j in up]
     above = lax.ppermute(last, "band", up)
     below = lax.ppermute(first, "band", down)
 
+    own, chosen = pl.pallas_call(
+        stage_kernel,
+        out_specs=[vmem, vmem],
+        out_shape=(
+            in_vmem((fields * rows, members_here, cols), f32),
+            in_vmem((patches, 3 * cells, nobs), bf16),
+        ),
+        cost_estimate=pl.CostEstimate(flops=10**8, bytes_accessed=10**6, transcendentals=0),
+        compiler_params=pltpu.CompilerParams(vmem_limit_bytes=24 * 1024 * 1024),
+        name="stage",
+    )(prior, obs_index[0])
+
     band = lax.axis_index("band")
     inside = jnp.stack([band > 0, band < bands - 1]).astype(f32)
-    vmem = pl.BlockSpec(memory_space=pltpu.VMEM)
-    smem = pl.BlockSpec(memory_space=pltpu.SMEM)
     deep = (fields * (rows + 2 * HALO), GROUP, cols)
     groups = members_here // GROUP
     per_group = GROUP * fields * rows * cols // LANES
-
-    def of_group(*shape):
-        return pl.BlockSpec(shape, lambda g: (0, g, 0))
 
     exact, sent = pl.pallas_call(
         forecast_kernel,
         grid=(groups,),
         in_specs=[
             smem,
-            pl.BlockSpec((per_group, LANES), lambda g: (g, 0)),
-            of_group(fields * HALO, GROUP, cols),
-            of_group(fields * HALO, GROUP, cols),
-            pl.BlockSpec((patches, nobs), lambda g: (0, 0)),
+            vmem,
+            vmem,
+            vmem,
+            vmem,
         ],
-        out_specs=[of_group(patches, GROUP, cells), of_group(patches, GROUP, cells + nobs)],
+        out_specs=[vmem, vmem],
         out_shape=(
-            shaped((patches, members_here, cells), f32),
-            shaped((patches, members_here, cells + nobs), bf16),
+            in_vmem((patches, members_here, cells), f32),
+            in_vmem((patches, members_here, cells + nobs), bf16),
         ),
         scratch_shapes=[pltpu.VMEM(deep, f32), pltpu.VMEM(deep, f32)],
+        compiler_params=pltpu.CompilerParams(vmem_limit_bytes=24 * 1024 * 1024),
         name="forecast",
-    )(inside, prior, above, below, obs_index[0])
+    )(inside, to_vmem(own), to_vmem(above), to_vmem(below), to_vmem(chosen))
 
     got = lax.all_to_all(sent, "mem", 0, 0, tiled=True).reshape(members, cells + nobs)
     here = lax.axis_index("mem").astype(jnp.int32).reshape(1)
     moved = pl.pallas_call(
         analyse_kernel,
         in_specs=[smem, vmem, vmem, vmem, vmem],
-        out_shape=shaped((patches, fields * members_here + 8, LANES), bf16),
+        out_specs=vmem,
+        out_shape=in_vmem((patches, fields * members_here + 8, LANES), bf16),
         name="analyse",
-    )(here, got, obs_index[0], obs_values[0], obs_var[0])
+    )(here, to_vmem(got), obs_index[0], obs_values[0], obs_var[0])
     returned = lax.all_to_all(moved, "mem", 0, 0, tiled=True)
     count = 2 * GROUP
     out = pl.pallas_call(
         unpack_kernel,
         grid=(members_here // count,),
         in_specs=[
-            pl.BlockSpec((patches, fields * members_here + 8, LANES), lambda g: (0, 0, 0)),
-            pl.BlockSpec((patches, count, cells), lambda g: (0, g, 0)),
+            vmem,
+            vmem,
         ],
         out_specs=pl.BlockSpec((2 * per_group, LANES), lambda g: (g, 0)),
         out_shape=shaped((members_here * fields * rows * cols // LANES, LANES), f32),
         name="unpack",
-    )(returned, exact)
+    )(to_vmem(returned), to_vmem(exact))
     return untiled_view(out, prior_collection.shape)
 
 

time: 99.2 us -> 92 us (0.927)
  waiting for transfers between devices: 22 us -> 18.1 us
  Pallas kernels: 24 us -> 21.1 us
    ppermute x1, waiting for transfers between devices: 2.05 us -> 0.01 us  [body(): above = lax.ppermute(last, 'band', up)]
    ppermute x1, waiting for transfers between devices: 1.86 us -> 0.01 us  [body(): below = lax.ppermute(first, 'band', down)]
    pallas_call x3 -> x4, Pallas kernels: 17.9 us -> 16.2 us  [the longest x1 10.4 us: body(): pl.pallas_call(forecast_kernel, grid=(groups,), in_specs=[smem, vmem, vme...]
    pallas_call x1, Pallas kernels: 6.08 us -> 4.92 us  [body(): pl.pallas_call(analyse_kernel, in_specs=[smem, vmem, vmem, vmem, vmem], o...]
  transfers between devices with their start and end apart: 3 -> 3, of which waited for: 3 -> 1; matrix products, arithmetic and copies ran while one was open for 1% -> 0% of each run, Pallas kernels for 0% -> 2%
where the time goes in v2:
time: 92 us; the launch traced here: 91.5 us
  starting transfers between devices  31.2 us (34%)
  Pallas kernels  21.1 us (23%)
  blocking collectives  19 us (21%)
  waiting for transfers between devices  18.1 us (20%)
  local copies, waits for them, and re-layouts  1.85 us (2%)
    all_to_all x1, blocking collectives, body(): returned = lax.all_to_all(moved, 'mem', 0, 0, tiled=True)  19 us
    all_to_all x1, waiting for transfers between devices, body(): lax.all_to_all(sent, 'mem', 0, 0, tiled=True).reshape(members, cells + nobs)  18.1 us
    ppermute x1, starting transfers between devices, body(): below = lax.ppermute(first, 'band', down)  16.7 us
    all_to_all x1, starting transfers between devices, body(): lax.all_to_all(sent, 'mem', 0, 0, tiled=True).reshape(members, cells + nobs)  12.6 us
    pallas_call x1, Pallas kernels, body(): pl.pallas_call(forecast_kernel, grid=(groups,), in_specs=[smem, vmem, vme...  10.4 us
    pallas_call x1, Pallas kernels, body(): pl.pallas_call(analyse_kernel, in_specs=[smem, vmem, vmem, vmem, vmem], o...  4.92 us
    pallas_call x1, Pallas kernels, body(): pl.pallas_call(stage_kernel, out_specs=[vmem, vmem], out_shape=(in_vmem((...  2.26 us
    pallas_call x1, Pallas kernels, body(): pl.pallas_call(unpack_kernel, grid=(members_here // count,), in_specs=[vm...  2.14 us
  transfers between devices with their start and end apart: 3, of which 1 were waited for; matrix products, arithmetic and copies ran while one was open for 0% of the time, Pallas kernels for 2%

profile of v2, /device:TPU:2, one launch (start us, length us, event | category | flops | bytes accessed | tf_op | source)
XLA Modules:
  0.0 91.5 jit_solution(9479231386391760709)
XLA Ops:
  0.0 1.4 %edges.1 = (bf16[18,32,256]{2,1,0:T(8,128)(2,1)S(1)}, bf16[18,32,256]{2,1,0:T(8,128)(2,1)S(1)}) custom-call(f32[1536,128]{1,0:T(8,128)} %bitcast.17), custom_call_target="tpu_custom_call" | custom-call | tf_op jit(solution)/shard_map/edges/pallas_call | solution.py:333
  1.4 1.9 %collective-permute-start = (bf16[18,32,256]{2,1,0:T(8,128)(2,1)S(1)}, bf16[18,32,256]{2,1,0:T(8,128)(2,1)S(1)}, u32[]{:S(2)}, u32[]{:S(2)}) collective-permute-start(bf16[18,32,256]{2,1,0:T(8,128)(2,1)S(1)} %get-tuple-element.12), channel_id=1, source_target_pairs={{0,1},{1,2},{2,3},{3,4},{4,5},{5,6},{6,7},{7,8},{8,9},{9,10},{10,1... | collective-permute-start | bytes 884744 | tf_op jit(solution)/shard_map/ppermute | solution.py:341
  3.3 16.7 %collective-permute-start.1 = (bf16[18,32,256]{2,1,0:T(8,128)(2,1)S(1)}, bf16[18,32,256]{2,1,0:T(8,128)(2,1)S(1)}, u32[]{:S(2)}, u32[]{:S(2)}) collective-permute-start(bf16[18,32,256]{2,1,0:T(8,128)(2,1)S(1)} %get-tuple-element.13), channel_id=1, source_target_pairs={{1,0},{2,1},{3,2},{4,3},{5,4},{6,5},{7,6},{8,7},{9,8},{10,9},{11,1... | collective-permute-start | bytes 884744 | tf_op jit(solution)/shard_map/ppermute | solution.py:342
  20.1 0.0 copy-start
  20.1 1.1 %copy-done = f32[32,3,8,256]{3,2,1,0:T(8,128)S(1)} copy-done((f32[32,3,8,256]{3,2,1,0:T(8,128)S(1)}, f32[32,3,8,256]{3,2,1,0:T(8,128)}, u32[]{:S(2)}) %copy-start) | copy-done | bytes 786456
  21.2 0.0 copy-start.1
  21.2 0.7 copy-done.1
  21.9 2.3 %stage.1 = (f32[24,32,256]{2,1,0:T(8,128)S(1)}, bf16[16,1152,256]{2,1,0:T(8,128)(2,1)S(1)}) custom-call(f32[1536,128]{1,0:T(8,128)S(1)} %bitcast.18, s32[16,256]{1,0:T(8,128)S(1)} %bitcast.21), custom_call_target="tpu_custom_call" | custom-call | flops 100000000 | bytes 1000000 | tf_op jit(solution)/shard_map/stage/pallas_call | solution.py:344
  24.2 0.1 add_convert_fusion.inside_ref
  24.3 0.0 collective-permute-done.above_ref
  24.3 0.0 collective-permute-done.1.below_ref
  24.3 10.4 %forecast.1 = (f32[16,32,384]{2,1,0:T(8,128)S(1)}, bf16[16,32,640]{2,1,0:T(8,128)(2,1)}) custom-call(f32[2]{0:T(128)S(1)} %add_convert_fusion.inside_ref, f32[24,32,256]{2,1,0:T(8,128)S(1)} %get-tuple-element.11.own_ref, bf16[18,32,256]{2,1,0:T(8,128)(2,1)S(1)} %collective-permute-done.above_ref, bf16[18,32,256]{2,1,0:T(8,128)(2,1)S(1)} %collective-permute-done.1.below_ref, ...), custom_call_target="tpu_custom_call" | custom-call | tf_op jit(solution)/shard_map/forecast/pallas_call | solution.py:362
  34.7 12.6 %all-to-all-start = ((bf16[16,32,640]{2,1,0:T(8,128)(2,1)}), bf16[16,32,640]{2,1,0:T(8,128)(2,1)S(1)}, u32[]{:S(2)}, u32[]{:S(2)}) async-start(bf16[16,32,640]{2,1,0:T(8,128)(2,1)} %get-tuple-element.15), calls=%async_computation | async-start | bytes 1310720 | tf_op jit(solution)/shard_map/all_to_all | solution.py:382
  47.3 18.1 %all-to-all-done = bf16[16,32,640]{2,1,0:T(8,128)(2,1)S(1)} async-done(((bf16[16,32,640]{2,1,0:T(8,128)(2,1)}), bf16[16,32,640]{2,1,0:T(8,128)(2,1)S(1)}, u32[]{:S(2)}, u32[]{:S(2)}) %all-to-all-start) | async-done | bytes 655392 | tf_op jit(solution)/shard_map/all_to_all | solution.py:382
  65.4 4.9 %analyse.1 = bf16[16,104,128]{2,1,0:T(8,128)(2,1)S(1)} custom-call(s32[1]{0:T(128)} %bitcast.here_ref, bf16[512,640]{1,0:T(8,128)(2,1)S(1)} %bitcast.19, s32[16,256]{1,0:T(8,128)} %bitcast.20, f32[1,256]{1,0:T(1,128)} %bitcast.22, f32[1,256]{1,0:T(1,128)} %bitcast.23), custom_call_target="tpu_custom_call" | custom-call | tf_op jit(solution)/shard_map/analyse/pallas_call | solution.py:384
  70.3 19.0 %all_to_all.10.returned_ref = bf16[16,104,128]{2,1,0:T(8,128)(2,1)S(1)} all-to-all(bf16[16,104,128]{2,1,0:T(8,128)(2,1)S(1)} %analyse.1), channel_id=1, replica_groups=mesh['mem'=16,'band'=64] {'mem'}, dimensions={0} | all-to-all | bytes 851968 | tf_op jit(solution)/shard_map/all_to_all | solution.py:391
  89.4 2.1 %unpack.1 = f32[1536,128]{1,0:T(8,128)} custom-call(bf16[16,104,128]{2,1,0:T(8,128)(2,1)S(1)} %all_to_all.10.returned_ref, f32[16,32,384]{2,1,0:T(8,128)S(1)} %get-tuple-element.16.exact_ref), custom_call_target="tpu_custom_call" | custom-call | tf_op jit(solution)/shard_map/unpack/pallas_call | solution.py:393
Async XLA Ops:
  1.4 22.9 %collective-permute-start = (bf16[18,32,256]{2,1,0:T(8,128)(2,1)S(1)}, bf16[18,32,256]{2,1,0:T(8,128)(2,1)S(1)}, u32[]{:S(2)}, u32[]{:S(2)}) collective-permute-start(bf16[18,32,256]{2,1,0:T(8,128)(2,1)S(1)} %get-tuple-element.12), channel_id=1, source_target_pairs={{0,1},{1,2},{2,3},{3,4},{4,5},{5,6},{6,7},{7,8},{8,9},{9,10},{10,1... | collective-permute-start | bytes 884744 | tf_op jit(solution)/shard_map/ppermute | solution.py:341
  3.3 21.0 %collective-permute-start.1 = (bf16[18,32,256]{2,1,0:T(8,128)(2,1)S(1)}, bf16[18,32,256]{2,1,0:T(8,128)(2,1)S(1)}, u32[]{:S(2)}, u32[]{:S(2)}) collective-permute-start(bf16[18,32,256]{2,1,0:T(8,128)(2,1)S(1)} %get-tuple-element.13), channel_id=1, source_target_pairs={{1,0},{2,1},{3,2},{4,3},{5,4},{6,5},{7,6},{8,7},{9,8},{10,9},{11,1... | collective-permute-start | bytes 884744 | tf_op jit(solution)/shard_map/ppermute | solution.py:342
  20.1 1.1 %copy-start = (f32[32,3,8,256]{3,2,1,0:T(8,128)S(1)}, f32[32,3,8,256]{3,2,1,0:T(8,128)}, u32[]{:S(2)}) copy-start(f32[32,3,8,256]{3,2,1,0:T(8,128)} %param.4) | copy-start | bytes 2359300
  21.2 0.7 copy-start.1
  34.7 30.7 %all-to-all-start = ((bf16[16,32,640]{2,1,0:T(8,128)(2,1)}), bf16[16,32,640]{2,1,0:T(8,128)(2,1)S(1)}, u32[]{:S(2)}, u32[]{:S(2)}) async-start(bf16[16,32,640]{2,1,0:T(8,128)(2,1)} %get-tuple-element.15), calls=%async_computation | async-start | bytes 1310720 | tf_op jit(solution)/shard_map/all_to_all | solution.py:382

commit v3 on v2

--- a/solution.py
+++ b/solution.py
@@ -56,7 +56,7 @@
     return tiles
 
 
-def edges_kernel(prior_ref, first_ref, last_ref):
+def edges_kernel(prior_ref, first_ref, last_ref, own_ref):
     fields, rows = 3, 8
     stride = fields * rows * 2
     for member in range(0, first_ref.shape[1], 2 * GROUP):
@@ -68,7 +68,9 @@
                         prior_ref[pl.ds((m * fields + f) * 2 * rows + half * rows + row, GROUP, stride=stride), :]
                         for m in (member, member + GROUP)
                     ]
-                    both = jnp.concatenate(parts, axis=0).astype(jnp.bfloat16)
+                    both = jnp.concatenate(parts, axis=0)
+                    own_ref[f * rows + row, member : member + 2 * GROUP, lanes] = both
+                    both = both.astype(jnp.bfloat16)
                     if row < HALO:
                         first_ref[f * HALO + row, member : member + 2 * GROUP, lanes] = both
                     if row >= rows - HALO:
@@ -81,17 +83,7 @@
     return (column >> 4) * (3 * LANES) + field_row * BLOCK + (column & (BLOCK - 1))
 
 
-def stage_kernel(prior_ref, index_ref, own_ref, chosen_ref):
-    fields, rows = 3, 8
-    stride = fields * rows * 2
-    for member in range(0, own_ref.shape[1], GROUP):
-        for f in range(fields):
-            for half in range(2):
-                for row in range(rows):
-                    start = (member * fields + f) * 2 * rows + half * rows + row
-                    own_ref[f * rows + row, member : member + GROUP, half * LANES : (half + 1) * LANES] = prior_ref[
-                        pl.ds(start, GROUP, stride=stride), :
-                    ]
+def stage_kernel(index_ref, chosen_ref):
     spots = window_spots(index_ref[...])
     order = lax.broadcasted_iota(jnp.int32, chosen_ref.shape[1:], 0)
     for p in range(chosen_ref.shape[0]):
@@ -103,13 +95,13 @@
     return pltpu.roll(x, cols - 1, 1) - pltpu.roll(x, 1, 1)
 
 
-def forecast_kernel(inside_ref, own_ref, above_ref, below_ref, chosen_ref, exact_ref, sent_ref, ping, pong):
+def forecast_kernel(place_ref, own_ref, above_ref, below_ref, chosen_ref, exact_ref, sent_ref, ping, pong):
     fields, rows = 3, 8
     deep = rows + 2 * HALO
     patches = sent_ref.shape[0]
     cells = fields * LANES
-    above_in = inside_ref[0]
-    below_in = inside_ref[1]
+    above_in = place_ref[0].astype(jnp.float32)
+    below_in = place_ref[1].astype(jnp.float32)
     half_step = 0.5 * time_step
     here = pl.ds(pl.multiple_of(pl.program_id(0) * GROUP, GROUP), GROUP)
 
@@ -213,13 +205,13 @@
     return stacked.astype(jnp.bfloat16)
 
 
-def analyse_kernel(here_ref, got_ref, index_ref, values_ref, var_ref, out_ref):
+def analyse_kernel(place_ref, got_ref, index_ref, values_ref, var_ref, out_ref):
     members = got_ref.shape[0]
     cells = got_ref.shape[1] - values_ref.shape[1]
     wide = got_ref[:, cells:].astype(jnp.float32)
     obs_mean = jnp.sum(wide, axis=0, keepdims=True) * (1.0 / members)
     perturb = (wide - obs_mean).astype(jnp.bfloat16)
-    index = index_ref[pl.ds(here_ref[0], 1), :]
+    index = index_ref[pl.ds(place_ref[2], 1), :]
     column = (index - ((index * 1366) >> 16) * (3 * BLOCK)).astype(jnp.float32)
     taper = jnp.exp(-0.5 * jnp.square((column - (3 * BLOCK - 1) * 0.5) / BLOCK))
     obs_weight = taper / var_ref[...]
@@ -330,10 +322,14 @@
     halo_shape = (fields * HALO, members_here, cols)
     vmem = pl.BlockSpec(memory_space=pltpu.VMEM)
     smem = pl.BlockSpec(memory_space=pltpu.SMEM)
-    first, last = pl.pallas_call(
+    first, last, own = pl.pallas_call(
         edges_kernel,
-        out_specs=[vmem, vmem],
-        out_shape=(in_vmem(halo_shape, bf16), in_vmem(halo_shape, bf16)),
+        out_specs=[vmem, vmem, vmem],
+        out_shape=(
+            in_vmem(halo_shape, bf16),
+            in_vmem(halo_shape, bf16),
+            in_vmem((fields * rows, members_here, cols), f32),
+        ),
         name="edges",
     )(prior)
     up = [(i, i + 1) for i in range(bands - 1)]
@@ -341,20 +337,17 @@
     above = lax.ppermute(last, "band", up)
     below = lax.ppermute(first, "band", down)
 
-    own, chosen = pl.pallas_call(
+    chosen = pl.pallas_call(
         stage_kernel,
-        out_specs=[vmem, vmem],
-        out_shape=(
-            in_vmem((fields * rows, members_here, cols), f32),
-            in_vmem((patches, 3 * cells, nobs), bf16),
-        ),
+        out_specs=vmem,
+        out_shape=in_vmem((patches, 3 * cells, nobs), bf16),
         cost_estimate=pl.CostEstimate(flops=10**8, bytes_accessed=10**6, transcendentals=0),
         compiler_params=pltpu.CompilerParams(vmem_limit_bytes=24 * 1024 * 1024),
         name="stage",
-    )(prior, obs_index[0])
+    )(obs_index[0])
 
     band = lax.axis_index("band")
-    inside = jnp.stack([band > 0, band < bands - 1]).astype(f32)
+    place = jnp.stack([band > 0, band < bands - 1, lax.axis_index("mem")]).astype(jnp.int32)
     deep = (fields * (rows + 2 * HALO), GROUP, cols)
     groups = members_here // GROUP
     per_group = GROUP * fields * rows * cols // LANES
@@ -377,17 +370,16 @@
         scratch_shapes=[pltpu.VMEM(deep, f32), pltpu.VMEM(deep, f32)],
         compiler_params=pltpu.CompilerParams(vmem_limit_bytes=24 * 1024 * 1024),
         name="forecast",
-    )(inside, to_vmem(own), to_vmem(above), to_vmem(below), to_vmem(chosen))
+    )(place, to_vmem(own), to_vmem(above), to_vmem(below), to_vmem(chosen))
 
     got = lax.all_to_all(sent, "mem", 0, 0, tiled=True).reshape(members, cells + nobs)
-    here = lax.axis_index("mem").astype(jnp.int32).reshape(1)
     moved = pl.pallas_call(
         analyse_kernel,
         in_specs=[smem, vmem, vmem, vmem, vmem],
         out_specs=vmem,
         out_shape=in_vmem((patches, fields * members_here + 8, LANES), bf16),
         name="analyse",
-    )(here, to_vmem(got), obs_index[0], obs_values[0], obs_var[0])
+    )(place, to_vmem(got), obs_index[0], obs_values[0], obs_var[0])
     returned = lax.all_to_all(moved, "mem", 0, 0, tiled=True)
     count = 2 * GROUP
     out = pl.pallas_call(

time: 92 us -> 90.8 us (0.987)
  blocking collectives: 19 us -> 49.5 us
  waiting for transfers between devices: 18.1 us -> 1.39 us
  starting transfers between devices: 31.2 us -> 18.6 us
  local copies, waits for them, and re-layouts: 1.85 us -> 0.72 us
  Pallas kernels: 21.1 us -> 20.1 us
    all_to_all x0 -> x1, blocking collectives: none -> 31.8 us  [body(): lax.all_to_all(sent, 'mem', 0, 0, tiled=True).reshape(members, cells + nobs)]
    all_to_all x1 -> x0, waiting for transfers between devices: 18.1 us -> none  [body(): lax.all_to_all(sent, 'mem', 0, 0, tiled=True).reshape(members, cells + nobs)]
    all_to_all x1 -> x0, starting transfers between devices: 12.6 us -> none  [body(): lax.all_to_all(sent, 'mem', 0, 0, tiled=True).reshape(members, cells + nobs)]
    ppermute x1, waiting for transfers between devices: 0.01 us -> 1.39 us  [body(): below = lax.ppermute(first, 'band', down)]
    all_to_all x1, blocking collectives: 19 us -> 17.7 us  [body(): returned = lax.all_to_all(moved, 'mem', 0, 0, tiled=True)]
    unnamed x4, local copies, waits for them, and re-layouts: 1.85 us -> 0.72 us
  transfers between devices with their start and end apart: 3 -> 2, of which waited for: 1 -> 1; matrix products, arithmetic and copies ran while one was open for 0% -> 0% of each run, Pallas kernels for 2% -> 2%
where the time goes in v3:
time: 90.8 us; the launch traced here: 90.5 us
  blocking collectives  49.5 us (55%)
  Pallas kernels  20.1 us (22%)
  starting transfers between devices  18.6 us (20%)
  waiting for transfers between devices  1.39 us (2%)
    all_to_all x1, blocking collectives, body(): lax.all_to_all(sent, 'mem', 0, 0, tiled=True).reshape(members, cells + nobs)  31.8 us
    all_to_all x1, blocking collectives, body(): returned = lax.all_to_all(moved, 'mem', 0, 0, tiled=True)  17.7 us
    ppermute x1, starting transfers between devices, body(): below = lax.ppermute(first, 'band', down)  16.7 us
    pallas_call x1, Pallas kernels, body(): pl.pallas_call(forecast_kernel, grid=(groups,), in_specs=[smem, vmem, vme...  9.52 us
    pallas_call x1, Pallas kernels, body(): pl.pallas_call(analyse_kernel, in_specs=[smem, vmem, vmem, vmem, vmem], o...  4.99 us
    pallas_call x1, Pallas kernels, body(): pl.pallas_call(unpack_kernel, grid=(members_here // count,), in_specs=[vm...  2.14 us
    pallas_call x1, Pallas kernels, body(): pl.pallas_call(stage_kernel, out_specs=vmem, out_shape=in_vmem((patches,...  2.01 us
    ppermute x1, starting transfers between devices, body(): above = lax.ppermute(last, 'band', up)  1.92 us
  transfers between devices with their start and end apart: 2, of which 1 were waited for; matrix products, arithmetic and copies ran while one was open for 0% of the time, Pallas kernels for 2%

profile of v3, /device:TPU:2, one launch (start us, length us, event | category | flops | bytes accessed | tf_op | source)
XLA Modules:
  0.0 90.5 jit_solution(11306078656020426769)
XLA Ops:
  0.0 1.4 %edges.1 = (bf16[18,32,256]{2,1,0:T(8,128)(2,1)S(1)}, bf16[18,32,256]{2,1,0:T(8,128)(2,1)S(1)}, f32[24,32,256]{2,1,0:T(8,128)S(1)}) custom-call(f32[1536,128]{1,0:T(8,128)} %bitcast.20), custom_call_target="tpu_custom_call" | custom-call | tf_op jit(solution)/shard_map/edges/pallas_call | solution.py:325
  1.4 1.9 %collective-permute-start = (bf16[18,32,256]{2,1,0:T(8,128)(2,1)S(1)}, bf16[18,32,256]{2,1,0:T(8,128)(2,1)S(1)}, u32[]{:S(2)}, u32[]{:S(2)}) collective-permute-start(bf16[18,32,256]{2,1,0:T(8,128)(2,1)S(1)} %get-tuple-element.11), channel_id=1, source_target_pairs={{0,1},{1,2},{2,3},{3,4},{4,5},{5,6},{6,7},{7,8},{8,9},{9,10},{10,1... | collective-permute-start | bytes 884744 | tf_op jit(solution)/shard_map/ppermute | solution.py:337
  3.4 16.7 %collective-permute-start.1 = (bf16[18,32,256]{2,1,0:T(8,128)(2,1)S(1)}, bf16[18,32,256]{2,1,0:T(8,128)(2,1)S(1)}, u32[]{:S(2)}, u32[]{:S(2)}) collective-permute-start(bf16[18,32,256]{2,1,0:T(8,128)(2,1)S(1)} %get-tuple-element.12), channel_id=1, source_target_pairs={{1,0},{2,1},{3,2},{4,3},{5,4},{6,5},{7,6},{8,7},{9,8},{10,9},{11,1... | collective-permute-start | bytes 884744 | tf_op jit(solution)/shard_map/ppermute | solution.py:338
  20.1 0.0 copy-start
  20.1 0.7 copy-done
  20.8 2.0 %stage.1.chosen_ref = bf16[16,1152,256]{2,1,0:T(8,128)(2,1)S(1)} custom-call(s32[16,256]{1,0:T(8,128)S(1)} %bitcast.19), custom_call_target="tpu_custom_call" | custom-call | flops 100000000 | bytes 1000000 | tf_op jit(solution)/shard_map/stage/pallas_call | solution.py:340
  22.8 0.1 pad_add_fusion.place_ref
  22.9 0.0 copy-start.1
  22.9 0.0 collective-permute-done.above_ref
  22.9 1.4 %collective-permute-done.1.below_ref = bf16[18,32,256]{2,1,0:T(8,128)(2,1)S(1)} collective-permute-done((bf16[18,32,256]{2,1,0:T(8,128)(2,1)S(1)}, bf16[18,32,256]{2,1,0:T(8,128)(2,1)S(1)}, u32[]{:S(2)}, u32[]{:S(2)}) %collective-permute-start.1) | collective-permute-done | bytes 294944 | tf_op jit(solution)/shard_map/ppermute | solution.py:338
  24.3 9.5 %forecast.1 = (f32[16,32,384]{2,1,0:T(8,128)S(1)}, bf16[16,32,640]{2,1,0:T(8,128)(2,1)S(1)}) custom-call(s32[3]{0:T(128)S(1)} %pad_add_fusion.place_ref, f32[24,32,256]{2,1,0:T(8,128)S(1)} %get-tuple-element.10.own_ref, bf16[18,32,256]{2,1,0:T(8,128)(2,1)S(1)} %collective-permute-done.above_ref, bf16[18,32,256]{2,1,0:T(8,128)(2,1)S(1)} %collective-permute-done.1.below_ref, ...), custom_call_target="tpu_custom_call" | custom-call | tf_op jit(solution)/shard_map/forecast/pallas_call | solution.py:355
  33.8 31.8 %all_to_all.10 = bf16[16,32,640]{2,1,0:T(8,128)(2,1)S(1)} all-to-all(bf16[16,32,640]{2,1,0:T(8,128)(2,1)S(1)} %get-tuple-element.13), channel_id=1, replica_groups=mesh['mem'=16,'band'=64] {'mem'}, dimensions={0} | all-to-all | bytes 1310720 | tf_op jit(solution)/shard_map/all_to_all | solution.py:375
  65.6 0.0 copy-done.1
  65.6 5.0 %analyse.1 = bf16[16,104,128]{2,1,0:T(8,128)(2,1)S(1)} custom-call(s32[3]{0:T(128)} %copy-done.1, bf16[512,640]{1,0:T(8,128)(2,1)S(1)} %bitcast.17, s32[16,256]{1,0:T(8,128)} %bitcast.18, f32[1,256]{1,0:T(1,128)} %bitcast.21, f32[1,256]{1,0:T(1,128)} %bitcast.22), custom_call_target="tpu_custom_call" | custom-call | tf_op jit(solution)/shard_map/analyse/pallas_call | solution.py:376
  70.6 17.7 %all_to_all.11.returned_ref = bf16[16,104,128]{2,1,0:T(8,128)(2,1)S(1)} all-to-all(bf16[16,104,128]{2,1,0:T(8,128)(2,1)S(1)} %analyse.1), channel_id=1, replica_groups=mesh['mem'=16,'band'=64] {'mem'}, dimensions={0} | all-to-all | bytes 851968 | tf_op jit(solution)/shard_map/all_to_all | solution.py:383
  88.3 2.1 %unpack.1 = f32[1536,128]{1,0:T(8,128)} custom-call(bf16[16,104,128]{2,1,0:T(8,128)(2,1)S(1)} %all_to_all.11.returned_ref, f32[16,32,384]{2,1,0:T(8,128)S(1)} %get-tuple-element.14.exact_ref), custom_call_target="tpu_custom_call" | custom-call | tf_op jit(solution)/shard_map/unpack/pallas_call | solution.py:385
Async XLA Ops:
  1.4 21.5 %collective-permute-start = (bf16[18,32,256]{2,1,0:T(8,128)(2,1)S(1)}, bf16[18,32,256]{2,1,0:T(8,128)(2,1)S(1)}, u32[]{:S(2)}, u32[]{:S(2)}) collective-permute-start(bf16[18,32,256]{2,1,0:T(8,128)(2,1)S(1)} %get-tuple-element.11), channel_id=1, source_target_pairs={{0,1},{1,2},{2,3},{3,4},{4,5},{5,6},{6,7},{7,8},{8,9},{9,10},{10,1... | collective-permute-start | bytes 884744 | tf_op jit(solution)/shard_map/ppermute | solution.py:337
  3.4 21.0 %collective-permute-start.1 = (bf16[18,32,256]{2,1,0:T(8,128)(2,1)S(1)}, bf16[18,32,256]{2,1,0:T(8,128)(2,1)S(1)}, u32[]{:S(2)}, u32[]{:S(2)}) collective-permute-start(bf16[18,32,256]{2,1,0:T(8,128)(2,1)S(1)} %get-tuple-element.12), channel_id=1, source_target_pairs={{1,0},{2,1},{3,2},{4,3},{5,4},{6,5},{7,6},{8,7},{9,8},{10,9},{11,1... | collective-permute-start | bytes 884744 | tf_op jit(solution)/shard_map/ppermute | solution.py:338
  20.1 0.7 copy-start
  22.9 42.7 %copy-start.1 = (s32[3]{0:T(128)}, s32[3]{0:T(128)S(1)}, u32[]{:S(2)}) copy-start(s32[3]{0:T(128)S(1)} %pad_add_fusion.place_ref) | copy-start | bytes 40
